TPU v7x, 512 devices: a whole 4x8x8 slice. The times are simulated.
512 devices in a mesh: row: 32 (over z, x), col: 16 (over y, core).
Axes of the slice: x: 4, y: 8, z: 8, core: 2. Of those that a mesh axis runs over, the one named last changes fastest.
Arguments:
- lower: bfloat16 [32, 3, 512, 2, 512], P('row', None, None, None, 'col'), as said below
- rhs: bfloat16 [32, 3, 512, 8192], P('row', None, None, 'col'), may hold values from -6 to 6
- tile_map: int32 [16], replicated, may hold values from 0 to 15, each once
Outputs:
- overwritten: bfloat16 [32, 3, 512, 8192], P('row', None, None, 'col')
Inputs may be any that keep to these rules, and one draw needn't show every extreme that they name: tile_map is a permutation of 0 to 15. lower[0, 0, :, 0, :] and lower[1, 0, :, 1, :] are lower triangular with diagonal entries between 2 and 3; lower[0, 0, :, 1, :] is zero.
All inputs are finite; a program needn't handle non-finite values.
Results may differ from a plain program's by a relative error of at most 0.0032.
Values may be sent and summed in bfloat16 or wider, within the bound.
A program may use at most 64 MiB of HBM per device.

v0:
```python
import jax
import jax.numpy as jnp
from jax import lax
from jax.sharding import Mesh
from jax.sharding import PartitionSpec as P

ROW = ("row_0", "row_1")


def spread(shard, axes, root):
    shard = jnp.where(lax.axis_index(axes) == root, shard, jnp.zeros_like(shard))
    for axis in axes:
        shard = lax.psum(shard, axis)
    return shard


def reorder(block, tile_map, tile):
    shape = block.shape
    tiles = block.reshape(shape[:-1] + (shape[-1] // tile, tile))
    return jnp.take(tiles, tile_map, axis=3).reshape(shape)


def body(lower, rhs, tile_map):
    tile = lower.shape[2]
    here = lax.axis_index(ROW)
    whole = lax.all_gather(lower, "col", axis=4, tiled=True)
    panels = whole[0]
    rows = panels.shape[0] * tile
    rhs = lax.all_to_all(
        reorder(
            lax.all_to_all(rhs, "col", split_axis=2, concat_axis=3, tiled=True), tile_map, tile
        ),
        "col",
        split_axis=3,
        concat_axis=2,
        tiled=True,
    )
    work = rhs[0].astype(jnp.float32)
    identity = jnp.eye(tile, dtype=jnp.float32)
    solved_rows = []
    for panel in range(2):
        mine = jnp.where(
            here == panel, jnp.tril(panels[0, :, panel, :].astype(jnp.float32)), identity
        )
        local = jax.scipy.linalg.solve_triangular(mine, work[0], lower=True).astype(jnp.bfloat16)
        solved = spread(local, ROW, panel)
        flat = panels[:, :, panel, :].reshape(rows, tile)
        work = work - jnp.dot(flat, solved, preferred_element_type=jnp.float32).reshape(work.shape)
        solved_rows.append(solved)
    first, second = (solved_rows[0], solved_rows[1])
    result = work.astype(jnp.bfloat16)
    leading = jnp.where(here == 0, first, jnp.where(here == 1, second, result[0]))
    result = result.at[0].set(leading)[None]
    return result


def solution(mesh):
    torus = Mesh(mesh.devices.reshape(8, 4, mesh.shape["col"]), ("row_0", "row_1", "col"))
    return jax.shard_map(
        body,
        mesh=torus,
        in_specs=(P(ROW, None, None, None, "col"), P(ROW, None, None, "col"), P()),
        out_specs=P(ROW, None, None, "col"),
        check_vma=False,
    )
```

profile of v0, /device:TPU:8, one launch (start us, length us, event | category | flops | bytes accessed | tf_op | source)
XLA Modules:
  0.0 522.2 jit_solution(17489380718761430764)
XLA Ops:
  6.5 4.1 copy.38
  10.6 9.4 %all-to-all-start = ((bf16[1,3,512,512]{3,1,0,2:T(4,128)(2,1)}), bf16[1,3,512,512]{3,1,0,2:T(4,128)(2,1)S(1)}, u32[]{:S(2)}, u32[]{:S(2)}) async-start(bf16[1,3,512,512]{3,1,0,2:T(4,128)(2,1)} %copy.38), calls=%async_computation | async-start | bytes 4194304 | tf_op jit(solution)/shard_map/all_to_all | solution.py:31
  20.1 0.9 copy.44
  21.2 56.9 %all-to-all-done = bf16[1,3,512,512]{3,1,0,2:T(4,128)(2,1)S(1)} async-done(((bf16[1,3,512,512]{3,1,0,2:T(4,128)(2,1)}), bf16[1,3,512,512]{3,1,0,2:T(4,128)(2,1)S(1)}, u32[]{:S(2)}, u32[]{:S(2)}) %all-to-all-start) | async-done | bytes 1572896 | tf_op jit(solution)/shard_map/all_to_all | solution.py:31
  78.1 1.5 copy.39
  79.6 2.1 gather_fusion
  81.6 0.9 copy.40
  82.5 0.8 gather.9
  83.5 8.3 %copy.41 = bf16[1,3,32,8192]{2,1,0,3:T(4,128)(2,1)} copy(bf16[1,3,32,8192]{3,2,1,0:T(8,128)(2,1)S(1)} %broadcast_select_fusion) | data formatting | bytes 3145728 | tf_op jit(solution)/shard_map/jit(_take)/select_n | solution.py:20
  91.8 13.2 %reshape.163 = bf16[16,2,24576]{2,1,0:T(2,128)(2,1)} reshape(bf16[8192,1,3,32]{3,2,1,0:T(4,128)(2,1)} %bitcast.122) | data formatting | bytes 3145728
  105.0 8.1 %all-to-all-start.1 = ((bf16[16,2,24576]{2,1,0:T(2,128)(2,1)}), bf16[16,2,24576]{2,1,0:T(2,128)(2,1)}, u32[]{:S(2)}, u32[]{:S(2)}) async-start(bf16[16,2,24576]{2,1,0:T(2,128)(2,1)} %reshape.163), calls=%async_computation.1 | async-start | bytes 3145728 | tf_op jit(solution)/shard_map/all_to_all | solution.py:29
  113.4 7.0 %copy.45 = bf16[1,3,512,2,512]{4,2,3,1,0:T(8,128)(2,1)S(1)} copy(bf16[1,3,512,2,512]{2,3,1,0,4:T(2,128)(2,1)} %all-gather.2.cloned.1.call-done) | data formatting | bytes 6291456 | tf_op jit(solution)/shard_map/all_gather | solution.py:26
  120.5 1.8 fusion.3
  122.7 11.5 %while.5 = (s32[]{:T(128)}, f32[512,512]{1,0:T(8,128)}, s32[4,2]{0,1:T(2,128)S(1)}, f32[4,128,128]{2,1,0:T(8,128)S(1)}, s32[]{:T(128)}) while((s32[]{:T(128)}, f32[512,512]{1,0:T(8,128)}, s32[4,2]{0,1:T(2,128)S(1)}, f32[4,128,128]{2,1,0:T(8,128)S(1)}, s32[]{:T(128)}) %tuple.41), condition=%wide.while_cond.1, body=%wide.while_body.1.sunk | while | flops 2 | bytes 131189 | solution.py:45
  123.4 2.3 bitcast_dynamic-update-slice_fusion.4
  126.3 2.3 bitcast_dynamic-update-slice_fusion.4
  129.2 2.3 bitcast_dynamic-update-slice_fusion.4
  132.1 2.2 bitcast_dynamic-update-slice_fusion.4
  134.3 39.3 %custom-call.4 = f32[4,128,128]{1,2,0:T(8,128)S(1)} custom-call(f32[4,128,128]{2,1,0:T(8,128)S(1)} %get-tuple-element.32), custom_call_target="InvertDiagBlocksLowerTriangular" | custom-call | tf_op jit(solution)/shard_map/jit(_solve_triangular)/triangular_solve | solution.py:45
  173.6 12.6 %reshape.164 = bf16[8192,1,3,32]{3,2,1,0:T(4,128)(2,1)} reshape(bf16[16,2,24576]{2,1,0:T(2,128)(2,1)} %all-to-all-done.1) | data formatting | bytes 3145728
  186.2 9.7 %copy.42 = bf16[1,3,32,8192]{3,2,1,0:T(8,128)(2,1)S(1)} copy(bf16[1,3,32,8192]{2,1,0,3:T(4,128)(2,1)} %bitcast.123) | data formatting | bytes 3145728 | tf_op jit(solution)/shard_map/all_to_all | solution.py:29
  197.2 0.9 copy-done.1
  198.5 1.2 convolution_subtract_fusion.3
  200.2 1.3 convolution_subtract_fusion.2
  202.0 1.6 convolution_subtract_fusion.5
  203.9 0.9 fusion.16
  204.9 83.1 %all-reduce.5.cloned.1.call-done = bf16[512,512]{1,0:T(8,128)(2,1)} async-done(((bf16[512,512]{1,0:T(8,128)(2,1)}), bf16[512,512]{1,0:T(8,128)(2,1)}) %all-reduce.5.cloned.1.call-update) | async-done | bytes 524304 | tf_op jit(solution)/shard_map/psum | solution.py:13
  289.0 13.6 %while.6 = (s32[]{:T(128)}, f32[512,512]{1,0:T(8,128)}, s32[4,2]{0,1:T(2,128)S(1)}, f32[4,128,128]{2,1,0:T(8,128)}, s32[]{:T(128)}) while((s32[]{:T(128)}, f32[512,512]{1,0:T(8,128)}, s32[4,2]{0,1:T(2,128)S(1)}, f32[4,128,128]{2,1,0:T(8,128)}, s32[]{:T(128)}) %tuple.57), condition=%wide.while_cond.1.clone, body=%wide.while_body.1.clone.sunk | while | flops 2 | bytes 132205 | solution.py:45
  289.6 2.8 bitcast_dynamic-update-slice_fusion.5
  293.0 2.8 bitcast_dynamic-update-slice_fusion.5
  296.4 2.8 bitcast_dynamic-update-slice_fusion.5
  299.8 2.7 bitcast_dynamic-update-slice_fusion.5
  302.6 3.7 copy.43
  306.3 40.1 %custom-call.5 = f32[4,128,128]{1,2,0:T(8,128)S(1)} custom-call(f32[4,128,128]{2,1,0:T(8,128)} %get-tuple-element.33), custom_call_target="InvertDiagBlocksLowerTriangular" | custom-call | tf_op jit(solution)/shard_map/jit(_solve_triangular)/triangular_solve | solution.py:45
  346.4 4.0 fusion.50
  350.4 4.3 convolution_bitcast_fusion.1
  354.7 3.6 copy.47
  358.2 2.6 sub.25
  361.4 1.3 convolution_subtract_fusion.1
  363.1 1.3 convolution_subtract_fusion
  364.9 1.6 convolution_subtract_fusion.4
  366.9 0.9 fusion.15
  368.1 77.8 %all-reduce.9.cloned.1.call-done = bf16[512,512]{1,0:T(8,128)(2,1)} async-done(((bf16[512,512]{1,0:T(8,128)(2,1)}), bf16[512,512]{1,0:T(8,128)(2,1)}) %all-reduce.9.cloned.1.call-update) | async-done | bytes 524304 | tf_op jit(solution)/shard_map/psum | solution.py:13
  445.9 54.0 %all-reduce.11.cloned.1.call-done = bf16[512,512]{1,0:T(8,128)(2,1)} async-done(((bf16[512,512]{1,0:T(8,128)(2,1)}), bf16[512,512]{1,0:T(8,128)(2,1)}) %all-reduce.11.cloned.1.call-update) | async-done | bytes 524304 | tf_op jit(solution)/shard_map/psum | solution.py:13
  499.9 4.3 convolution_bitcast_fusion
  504.2 3.6 copy.50
  507.8 5.2 fusion.1
  513.0 2.7 fusion.21
  (64 shorter events, 12.0 us)
Async XLA Ops:
  10.6 9.5 %copy-start.5 = (bf16[1,3,512,2,32]{2,4,3,1,0:T(8,128)(2,1)S(1)}, bf16[1,3,512,2,32]{2,4,3,1,0:T(8,128)(2,1)}, u32[]{:S(2)}) copy-start(bf16[1,3,512,2,32]{2,4,3,1,0:T(8,128)(2,1)} %param.7) | copy-start | bytes 589828
  10.6 10.4 %copy-start.6 = (s32[16]{0:T(128)S(1)}, s32[16]{0:T(128)}, u32[]{:S(2)}) copy-start(s32[16]{0:T(128)} %param.9) | copy-start | bytes 196
  10.6 67.4 %all-to-all-start = ((bf16[1,3,512,512]{3,1,0,2:T(4,128)(2,1)}), bf16[1,3,512,512]{3,1,0,2:T(4,128)(2,1)S(1)}, u32[]{:S(2)}, u32[]{:S(2)}) async-start(bf16[1,3,512,512]{3,1,0,2:T(4,128)(2,1)} %copy.38), calls=%async_computation | async-start | bytes 4194304 | tf_op jit(solution)/shard_map/all_to_all | solution.py:31
  20.1 93.4 %all-gather.2.cloned.1.call-start = ((), (), s32[]{:S(2)}) async-start(), calls=%async_computation.2 | async-start | bytes 3342336 | tf_op jit(solution)/shard_map/all_gather | solution.py:26
  105.0 68.5 %all-to-all-start.1 = ((bf16[16,2,24576]{2,1,0:T(2,128)(2,1)}), bf16[16,2,24576]{2,1,0:T(2,128)(2,1)}, u32[]{:S(2)}, u32[]{:S(2)}) async-start(bf16[16,2,24576]{2,1,0:T(2,128)(2,1)} %reshape.163), calls=%async_computation.1 | async-start | bytes 3145728 | tf_op jit(solution)/shard_map/all_to_all | solution.py:29
  113.2 174.8 %all-reduce.5.cloned.1.call-start = ((), (), s32[]{:S(2)}) async-start(), calls=%async_computation.3 | async-start | bytes 1048576 | tf_op jit(solution)/shard_map/psum | solution.py:13
  120.5 2.2 copy-start
  196.5 1.7 copy-start.1
  204.9 145.5 %all-reduce.7.cloned.1.call-start = ((), (), s32[]{:S(2)}) async-start(), calls=%async_computation.4 | async-start | bytes 1048576 | tf_op jit(solution)/shard_map/psum | solution.py:13
  288.0 157.9 %all-reduce.9.cloned.1.call-start = ((), (), s32[]{:S(2)}) async-start(), calls=%async_computation.5 | async-start | bytes 1048576 | tf_op jit(solution)/shard_map/psum | solution.py:13
  360.9 1.8 copy-start.2
  367.8 132.1 %all-reduce.11.cloned.1.call-start = ((), (), s32[]{:S(2)}) async-start(), calls=%async_computation.6 | async-start | bytes 1048576 | tf_op jit(solution)/shard_map/psum | solution.py:13
  507.8 5.2 copy-start.3
  507.8 5.2 copy-start.4
Sparse Core Ops, SparseCore 0:
  23.0 65.0 all-gather.1
  205.0 82.9 all-reduce.4
  290.4 51.8 all-reduce.6
  367.9 77.9 all-reduce.8
  448.1 51.7 all-reduce.10
where the time goes:
time: 524 us; the launch traced here: 522 us
  waiting for transfers between devices  272 us (52%)
  local copies, waits for them, and re-layouts  104 us (20%)
  other arithmetic  93.7 us (18%)
  matrix products  20.2 us (4%)
  starting transfers between devices  18.4 us (4%)
  between operations  13.5 us (3%)
    psum x4, waiting for transfers between devices, spread(): shard = lax.psum(shard, axis)  215 us
    another operation x4, other arithmetic, body(): jax.scipy.linalg.solve_triangular(mine, work[0], lower=True)  81.2 us
    all_to_all x1, waiting for transfers between devices, body(): lax.all_to_all(rhs, 'col', split_axis=2, concat_axis=3, tiled=True)  56.9 us
    unnamed x21, local copies, waits for them, and re-layouts  32.9 us
    another operation x27, local copies, waits for them, and re-layouts, body(): jax.scipy.linalg.solve_triangular(mine, work[0], lower=True)  25.7 us
    another operation x14, matrix products, body(): jax.scipy.linalg.solve_triangular(mine, work[0], lower=True)  11.6 us
  transfers between devices with their start and end apart: 7, of which 4 were waited for; matrix products, arithmetic and copies ran while one was open for 29% of the time, Pallas kernels for 0%

commit v1 on v0

--- a/solution.py
+++ b/solution.py
@@ -10,7 +10,7 @@
 def spread(shard, axes, root):
     shard = jnp.where(lax.axis_index(axes) == root, shard, jnp.zeros_like(shard))
     for axis in axes:
-        shard = lax.psum(shard, axis)
+        shard = jnp.sum(lax.all_gather(shard, axis), axis=0)
     return shard
 
 

time: 524 us -> 473 us (0.903)
  the two profiles are of different devices: /device:TPU:8 before, /device:TPU:1 now
where the time goes in v1:
time: 473 us; the launch traced here: 471 us
  waiting for transfers between devices  210 us (44%)
  other arithmetic  107 us (23%)
  local copies, waits for them, and re-layouts  102 us (22%)
  matrix products  20.3 us (4%)
  starting transfers between devices  17.6 us (4%)
  between operations  13.5 us (3%)
    all_gather x4, waiting for transfers between devices, spread(): shard = jnp.sum(lax.all_gather(shard, axis), axis=0)  151 us
    another operation x4, other arithmetic, body(): jax.scipy.linalg.solve_triangular(mine, work[0], lower=True)  81.2 us
    all_to_all x1, waiting for transfers between devices, body(): lax.all_to_all(rhs, 'col', split_axis=2, concat_axis=3, tiled=True)  58.8 us
    unnamed x23, local copies, waits for them, and re-layouts  33.6 us
    another operation x27, local copies, waits for them, and re-layouts, body(): jax.scipy.linalg.solve_triangular(mine, work[0], lower=True)  22.8 us
    reduce_sum x4, other arithmetic, spread(): shard = jnp.sum(lax.all_gather(shard, axis), axis=0)  13.2 us
    another operation x14, matrix products, body(): jax.scipy.linalg.solve_triangular(mine, work[0], lower=True)  11.6 us
    all_to_all x1, starting transfers between devices, body(): lax.all_to_all(rhs, 'col', split_axis=2, concat_axis=3, tiled=True)  10.5 us
  transfers between devices with their start and end apart: 7, of which 4 were waited for; matrix products, arithmetic and copies ran while one was open for 31% of the time, Pallas kernels for 0%

profile of v1, /device:TPU:1, one launch (start us, length us, event | category | flops | bytes accessed | tf_op | source)
XLA Modules:
  0.0 470.9 jit_solution(5780092272472809311)
XLA Ops:
  6.5 4.1 copy.51
  10.6 10.5 %all-to-all-start = ((bf16[1,3,512,512]{3,1,0,2:T(4,128)(2,1)}), bf16[1,3,512,512]{3,1,0,2:T(4,128)(2,1)S(1)}, u32[]{:S(2)}, u32[]{:S(2)}) async-start(bf16[1,3,512,512]{3,1,0,2:T(4,128)(2,1)} %copy.51), calls=%async_computation | async-start | bytes 4194304 | tf_op jit(solution)/shard_map/all_to_all | solution.py:31
  22.2 58.8 %all-to-all-done = bf16[1,3,512,512]{3,1,0,2:T(4,128)(2,1)S(1)} async-done(((bf16[1,3,512,512]{3,1,0,2:T(4,128)(2,1)}), bf16[1,3,512,512]{3,1,0,2:T(4,128)(2,1)S(1)}, u32[]{:S(2)}, u32[]{:S(2)}) %all-to-all-start) | async-done | bytes 1572896 | tf_op jit(solution)/shard_map/all_to_all | solution.py:31
  81.0 1.5 copy.52
  82.5 2.1 gather_fusion
  86.4 8.3 %copy.54 = bf16[1,3,32,8192]{2,1,0,3:T(4,128)(2,1)} copy(bf16[1,3,32,8192]{3,2,1,0:T(8,128)(2,1)S(1)} %broadcast_select_fusion) | data formatting | bytes 3145728 | tf_op jit(solution)/shard_map/jit(_take)/select_n | solution.py:20
  94.7 13.2 %reshape.182 = bf16[16,2,24576]{2,1,0:T(2,128)(2,1)} reshape(bf16[8192,1,3,32]{3,2,1,0:T(4,128)(2,1)} %bitcast.124) | data formatting | bytes 3145728
  107.9 6.2 %all-to-all-start.1 = ((bf16[16,2,24576]{2,1,0:T(2,128)(2,1)}), bf16[16,2,24576]{2,1,0:T(2,128)(2,1)}, u32[]{:S(2)}, u32[]{:S(2)}) async-start(bf16[16,2,24576]{2,1,0:T(2,128)(2,1)} %reshape.182), calls=%async_computation.1 | async-start | bytes 3145728 | tf_op jit(solution)/shard_map/all_to_all | solution.py:29
  114.5 7.0 %copy.58 = bf16[1,3,512,2,512]{4,2,3,1,0:T(8,128)(2,1)S(1)} copy(bf16[1,3,512,2,512]{2,3,1,0,4:T(2,128)(2,1)} %all-gather.10.cloned.1.call-done) | data formatting | bytes 6291456 | tf_op jit(solution)/shard_map/all_gather | solution.py:26
  121.5 1.8 fusion.3
  123.7 11.6 %while.5 = (s32[]{:T(128)}, f32[512,512]{1,0:T(8,128)}, s32[4,2]{0,1:T(2,128)S(1)}, f32[4,128,128]{2,1,0:T(8,128)S(1)}, s32[]{:T(128)}) while((s32[]{:T(128)}, f32[512,512]{1,0:T(8,128)}, s32[4,2]{0,1:T(2,128)S(1)}, f32[4,128,128]{2,1,0:T(8,128)S(1)}, s32[]{:T(128)}) %tuple.41), condition=%wide.while_cond.1, body=%wide.while_body.1.sunk | while | flops 2 | bytes 131189 | solution.py:45
  124.4 2.3 bitcast_dynamic-update-slice_fusion.4
  127.3 2.3 bitcast_dynamic-update-slice_fusion.4
  130.3 2.3 bitcast_dynamic-update-slice_fusion.4
  133.2 2.2 bitcast_dynamic-update-slice_fusion.4
  135.4 39.3 %custom-call.4 = f32[4,128,128]{1,2,0:T(8,128)S(1)} custom-call(f32[4,128,128]{2,1,0:T(8,128)S(1)} %get-tuple-element.32), custom_call_target="InvertDiagBlocksLowerTriangular" | custom-call | tf_op jit(solution)/shard_map/jit(_solve_triangular)/triangular_solve | solution.py:45
  174.7 12.6 %reshape.183 = bf16[8192,1,3,32]{3,2,1,0:T(4,128)(2,1)} reshape(bf16[16,2,24576]{2,1,0:T(2,128)(2,1)} %all-to-all-done.1) | data formatting | bytes 3145728
  187.3 9.7 %copy.55 = bf16[1,3,32,8192]{3,2,1,0:T(8,128)(2,1)S(1)} copy(bf16[1,3,32,8192]{2,1,0,3:T(4,128)(2,1)} %bitcast.125) | data formatting | bytes 3145728 | tf_op jit(solution)/shard_map/all_to_all | solution.py:29
  198.3 1.0 copy-done.1
  199.7 1.2 convolution_subtract_fusion.3
  201.3 1.3 convolution_subtract_fusion.2
  203.1 1.6 convolution_subtract_fusion.5
  206.1 61.0 %all-gather.12.cloned.1.call-done = bf16[4096,512]{1,0:T(8,128)(2,1)} async-done(((bf16[512,512]{1,0:T(8,128)(2,1)}), bf16[4096,512]{1,0:T(8,128)(2,1)}) %all-gather.12.cloned.1.call-update) | async-done | bytes 4194320 | tf_op jit(solution)/shard_map/all_gather | solution.py:13
  267.1 3.7 reduce_sum.52
  271.1 3.7 copy.56
  274.9 11.3 %while.6 = (s32[]{:T(128)}, f32[512,512]{1,0:T(8,128)}, s32[4,2]{0,1:T(2,128)S(1)}, f32[4,128,128]{2,1,0:T(8,128)S(1)}, s32[]{:T(128)}) while((s32[]{:T(128)}, f32[512,512]{1,0:T(8,128)}, s32[4,2]{0,1:T(2,128)S(1)}, f32[4,128,128]{2,1,0:T(8,128)S(1)}, s32[]{:T(128)}) %tuple.57), condition=%wide.while_cond.1.clone, body=%wide.while_body.1.clone.sunk | while | flops 2 | bytes 131189 | solution.py:45
  275.5 2.2 bitcast_dynamic-update-slice_fusion.5
  278.3 2.2 bitcast_dynamic-update-slice_fusion.5
  281.1 2.2 bitcast_dynamic-update-slice_fusion.5
  284.0 2.2 bitcast_dynamic-update-slice_fusion.5
  286.9 40.1 %custom-call.5 = f32[4,128,128]{1,2,0:T(8,128)S(1)} custom-call(f32[4,128,128]{2,1,0:T(8,128)} %copy-done.5), custom_call_target="InvertDiagBlocksLowerTriangular" | custom-call | tf_op jit(solution)/shard_map/jit(_solve_triangular)/triangular_solve | solution.py:45
  327.0 4.0 fusion.49
  330.9 2.9 reduce_sum.53
  333.8 4.3 convolution_bitcast_fusion.1
  338.1 3.6 copy.60
  341.7 2.6 sub.25
  344.9 1.3 convolution_subtract_fusion.1
  346.6 1.3 convolution_subtract_fusion
  348.4 1.6 convolution_subtract_fusion.4
  350.4 0.9 fusion.15
  351.6 56.1 %all-gather.16.cloned.1.call-done = bf16[4096,512]{1,0:T(8,128)(2,1)} async-done(((bf16[512,512]{1,0:T(8,128)(2,1)}), bf16[4096,512]{1,0:T(8,128)(2,1)}) %all-gather.16.cloned.1.call-update) | async-done | bytes 4194320 | tf_op jit(solution)/shard_map/all_gather | solution.py:13
  407.7 3.7 reduce_sum.54
  411.4 34.3 %all-gather.18.cloned.1.call-done = bf16[2048,512]{1,0:T(8,128)(2,1)} async-done(((bf16[512,512]{1,0:T(8,128)(2,1)}), bf16[2048,512]{1,0:T(8,128)(2,1)}) %all-gather.18.cloned.1.call-update) | async-done | bytes 2097168 | tf_op jit(solution)/shard_map/all_gather | solution.py:13
  445.8 2.9 reduce_sum.55
  448.6 4.4 convolution_bitcast_fusion
  453.0 3.5 copy.63
  456.5 5.2 %fusion.1 = bf16[1,3,512,512]{3,2,1,0:T(8,128)(2,1)} fusion(f32[1,3,512,512]{3,2,1,0:T(8,128)} %bitcast.133, f32[1,3,512,512]{3,2,1,0:T(8,128)} %bitcast.128, f32[1,3,16,32,512]{4,3,2,1,0:T(8,128)S(1)} %copy.56), kind=kLoop, calls=%fused_computation.9 | loop fusion | flops 2359296 | bytes 11010048 | tf_op jit(solution)/shard_map/convert_element_type | solution.py:51
  461.7 2.7 fusion.20
  (70 shorter events, 15.6 us)
Async XLA Ops:
  10.6 10.5 %copy-start.6 = (bf16[1,3,512,2,32]{2,4,3,1,0:T(8,128)(2,1)S(1)}, bf16[1,3,512,2,32]{2,4,3,1,0:T(8,128)(2,1)}, u32[]{:S(2)}) copy-start(bf16[1,3,512,2,32]{2,4,3,1,0:T(8,128)(2,1)} %param.7) | copy-start | bytes 589828
  10.6 11.4 %copy-start.7 = (s32[16]{0:T(128)S(1)}, s32[16]{0:T(128)}, u32[]{:S(2)}) copy-start(s32[16]{0:T(128)} %param.9) | copy-start | bytes 196
  10.6 70.3 %all-to-all-start = ((bf16[1,3,512,512]{3,1,0,2:T(4,128)(2,1)}), bf16[1,3,512,512]{3,1,0,2:T(4,128)(2,1)S(1)}, u32[]{:S(2)}, u32[]{:S(2)}) async-start(bf16[1,3,512,512]{3,1,0,2:T(4,128)(2,1)} %copy.51), calls=%async_computation | async-start | bytes 4194304 | tf_op jit(solution)/shard_map/all_to_all | solution.py:31
  21.1 93.4 %all-gather.10.cloned.1.call-start = ((), (), s32[]{:S(2)}) async-start(), calls=%async_computation.2 | async-start | bytes 3342336 | tf_op jit(solution)/shard_map/all_gather | solution.py:26
  107.9 66.8 %all-to-all-start.1 = ((bf16[16,2,24576]{2,1,0:T(2,128)(2,1)}), bf16[16,2,24576]{2,1,0:T(2,128)(2,1)}, u32[]{:S(2)}, u32[]{:S(2)}) async-start(bf16[16,2,24576]{2,1,0:T(2,128)(2,1)} %reshape.182), calls=%async_computation.1 | async-start | bytes 3145728 | tf_op jit(solution)/shard_map/all_to_all | solution.py:29
  114.2 152.9 %all-gather.12.cloned.1.call-start = ((), (), s32[]{:S(2)}) async-start(), calls=%async_computation.3 | async-start | bytes 4718592 | tf_op jit(solution)/shard_map/all_gather | solution.py:13
  121.5 2.2 copy-start
  197.6 1.7 copy-start.1
  206.0 124.9 %all-gather.14.cloned.1.call-start = ((), (), s32[]{:S(2)}) async-start(), calls=%async_computation.4 | async-start | bytes 2621440 | tf_op jit(solution)/shard_map/all_gather | solution.py:13
  270.9 136.8 %all-gather.16.cloned.1.call-start = ((), (), s32[]{:S(2)}) async-start(), calls=%async_computation.5 | async-start | bytes 4718592 | tf_op jit(solution)/shard_map/all_gather | solution.py:13
  286.2 0.7 copy-start.5
  344.3 1.8 copy-start.2
  351.3 94.5 %all-gather.18.cloned.1.call-start = ((), (), s32[]{:S(2)}) async-start(), calls=%async_computation.6 | async-start | bytes 2621440 | tf_op jit(solution)/shard_map/all_gather | solution.py:13
  456.5 5.2 %copy-start.3 = (bf16[512,512]{1,0:T(8,128)(2,1)S(1)}, bf16[512,512]{1,0:T(8,128)(2,1)}, u32[]{:S(2)}) copy-start(bf16[512,512]{1,0:T(8,128)(2,1)} %reduce_sum.53) | copy-start | bytes 1572868
  456.5 5.2 %copy-start.4 = (bf16[512,512]{1,0:T(8,128)(2,1)S(1)}, bf16[512,512]{1,0:T(8,128)(2,1)}, u32[]{:S(2)}) copy-start(bf16[512,512]{1,0:T(8,128)(2,1)} %reduce_sum.55) | copy-start | bytes 1572868
Sparse Core Ops, SparseCore 0:
  24.0 65.5 all-gather.9
  206.1 60.9 all-gather.11
  271.0 34.1 all-gather.13
  351.4 56.2 all-gather.15
  411.6 34.1 all-gather.17
